TPU v7x, 256 devices: a whole 4x4x8 slice. The times are simulated.
256 devices in a mesh: nodes: 128 (over y, z, x), feat: 2 (over core).
Axes of the slice: x: 4, y: 4, z: 8, core: 2. Of those that a mesh axis runs over, the one named last changes fastest.
Arguments:
- features: bfloat16 [65536, 128], P('nodes'), may hold values from -6 to 6
- row_counts: int32 [128], P('nodes'), may hold values from 128 to 512, as said below
- send_rows: int32 [128, 128, 64], P('nodes'), may hold values from 0 to 511, as said below
- edge_src: int32 [2, 524288], P(None, 'nodes'), may hold values from 0 to 8703, as said below
- edge_dst: int32 [2, 524288], P(None, 'nodes'), may hold values from 0 to 511, as said below
- edge_keep: int32 [2, 524288], P(None, 'nodes'), may hold values 0 or 1
- w_first: bfloat16 [128, 512], P(None, 'feat'), may hold values from -0.5 to 0.5
- b_first: float32 [512], P('feat'), may hold values from -3 to 3
- w_second: bfloat16 [512, 512], P(None, 'feat'), may hold values from -0.25 to 0.25
Outputs:
- normed: bfloat16 [2, 65536, 512], P(None, 'nodes', 'feat')
- correlation: float32 [512, 512], P('nodes', 'feat')
- barlow_loss: float32 [], replicated
Inputs may be any that keep to these rules, and one draw needn't show every extreme that they name: `row_counts`: some partition has all 512 rows live. send_rows[i, j, h] is below row_counts[i]. `edge_src`: A source below 512 is below row_counts of the edge's partition. `edge_dst`: A partition's edge slots come in aligned blocks of 1024 slots; block k targets rows k * 128 to (k + 1) * 128 - 1.
All inputs are finite; a program needn't handle non-finite values. No bound on the sum of `edge_keep` on one device may be relied on, other than what follows from the above.
Results may differ from a plain program's by a relative error of at most 0.0017.
The roundings to bfloat16 on the way count: a program that leaves them out, or rounds other values in their place, can miss the bound.
Values may be sent and summed in bfloat16 or wider, within the bound.
No kernel may reach another device: no remote copies, remote signals or barrier semaphores. Data moves between devices by JAX's collectives and lax.ppermute only.
A program may use at most 64 MiB of HBM per device.

v0:
```python
import jax
import jax.numpy as jnp
from jax import lax
from jax.sharding import Mesh
from jax.sharding import PartitionSpec as P

NODES = ("nodes_0", "nodes_1", "nodes_2")
NODES_FEAT = ("nodes_0", "nodes_1", "nodes_2", "feat")


def joined_along(tiles, dim):
    shape = list(tiles.shape[1:])
    shape[dim] *= tiles.shape[0]
    return jnp.moveaxis(tiles, 0, dim).reshape(shape)


def from_everyone(shard, axis):
    devices = lax.axis_size(axis)
    return lax.all_to_all(
        jnp.broadcast_to(shard[None], (devices, *shard.shape)), axis, 0, 0, tiled=True
    )


def gathered_copies(shard, axis, dim):
    return joined_along(from_everyone(shard, axis), dim)


def over_axes(shard, axes):
    for axis in axes:
        shard = lax.psum(shard, axis)
    return shard


def own_rows(running, axes):
    for axis in axes:
        running = lax.psum_scatter(running, axis, scatter_dimension=0, tiled=True)
    return running


def per_device(
    features, row_counts, send_rows, edge_src, edge_dst, edge_keep, w_first, b_first, w_second
):
    local_rows = features.shape[0]
    partitions = lax.axis_size(NODES)
    halo_rows = send_rows.shape[2]
    edge_total = edge_src.shape[1]
    tile_rows = min(128, local_rows)
    tiles = local_rows // tile_rows
    per_tile = edge_total // tiles
    live_rows = (jnp.arange(local_rows) < row_counts[0]).astype(jnp.float32)[:, None]
    kept_edges = edge_keep.astype(jnp.float32)
    outbound = send_rows[0]
    tile_base = (jnp.arange(tiles, dtype=jnp.int32) * tile_rows)[:, None]
    row_slots = jnp.arange(tile_rows, dtype=jnp.int32)
    tables = []
    degrees = []
    for view_index in range(2):
        inside = edge_dst[view_index].reshape(tiles, per_tile) - tile_base
        table = (inside[:, :, None] == row_slots[None, None, :]).astype(jnp.float32) * kept_edges[
            view_index
        ].reshape(tiles, per_tile)[:, :, None]
        tables.append(table)
        degrees.append(jnp.sum(table, 1).reshape(local_rows))

    def mix_view(lookup, view_index):
        width = lookup.shape[1]
        picked = lookup[edge_src[view_index]].astype(jnp.float32).reshape(tiles, per_tile, width)
        summed = jnp.einsum(
            "tes,tec->tsc",
            tables[view_index],
            picked,
            precision=lax.Precision.HIGHEST,
            preferred_element_type=jnp.float32,
        )
        summed = summed.reshape(local_rows, width)
        return (lookup[:local_rows].astype(jnp.float32) + summed) / (1.0 + degrees[view_index])[
            :, None
        ]

    arrived = lax.all_to_all(features[outbound], NODES, split_axis=0, concat_axis=0, tiled=True)
    lookup = jnp.concatenate([features, arrived.reshape(partitions * halo_rows, -1)], 0)
    weights_wide = w_first.astype(jnp.float32)
    averaged = [
        jnp.dot(mix_view(lookup, view_index), weights_wide, precision=lax.Precision.HIGHEST)
        for view_index in range(2)
    ]
    hidden = jnp.stack([jax.nn.relu(branch + b_first) for branch in averaged]).astype(jnp.bfloat16)
    summed_second = jnp.einsum(
        "gnq,qm->gnm",
        gathered_copies(hidden, "feat", 2),
        w_second,
        preferred_element_type=jnp.float32,
    )
    projected = summed_second.astype(jnp.bfloat16)
    arrived_second = lax.all_to_all(
        projected[:, outbound], NODES, split_axis=1, concat_axis=1, tiled=True
    )
    embedded = jnp.stack(
        [
            mix_view(
                jnp.concatenate(
                    [
                        projected[view_index],
                        arrived_second[view_index].reshape(partitions * halo_rows, -1),
                    ],
                    0,
                ),
                view_index,
            )
            for view_index in range(2)
        ]
    )
    column_sums, squares, node_total = (
        over_axes(jnp.sum(embedded * live_rows, 1), NODES),
        over_axes(jnp.sum(jnp.square(embedded) * live_rows, 1), NODES),
        over_axes(row_counts[0].astype(jnp.float32), NODES),
    )
    average = column_sums / node_total
    variance = squares / node_total - jnp.square(average)
    normed = (
        (embedded - average[:, None, :]) / jnp.sqrt(variance + 1e-05)[:, None, :] * live_rows
    ).astype(jnp.bfloat16)
    wide_first = gathered_copies(normed[0], "feat", 1)
    row_share = wide_first.shape[1] // partitions
    contract_rows = (((0,), (0,)), ((), ()))
    owned_rows = own_rows(
        lax.dot_general(wide_first, normed[1], contract_rows, preferred_element_type=jnp.float32),
        NODES,
    )
    correlation = owned_rows / node_total
    own_columns = correlation.shape[1]
    row_labels = lax.axis_index(NODES) * row_share + jnp.arange(row_share, dtype=jnp.int32)[:, None]
    column_labels = (
        lax.axis_index("feat") * own_columns + jnp.arange(own_columns, dtype=jnp.int32)[None, :]
    )
    partial_loss = jnp.sum(
        jnp.where(
            row_labels == column_labels,
            jnp.square(1.0 - correlation),
            0.005 * jnp.square(correlation),
        )
    )
    barlow_loss = over_axes(partial_loss, NODES_FEAT)
    return (normed, correlation, barlow_loss)


def solution(mesh):
    torus = Mesh(
        mesh.devices.reshape(4, 8, 4, mesh.shape["feat"]), ("nodes_0", "nodes_1", "nodes_2", "feat")
    )
    placed = (
        P(NODES, None),
        P(NODES),
        P(NODES, None, None),
        P(None, NODES),
        P(None, NODES),
        P(None, NODES),
        P(None, "feat"),
        P("feat"),
        P(None, "feat"),
    )
    return jax.shard_map(
        per_device,
        mesh=torus,
        in_specs=placed,
        out_specs=(P(None, NODES, "feat"), P(NODES, "feat"), P()),
        check_vma=False,
    )
```

profile of v0, /device:TPU:1, one launch (start us, length us, event | category | flops | bytes accessed | tf_op | source)
XLA Modules:
  0.0 631.1 jit_solution(14449898697765373779)
XLA Ops:
  7.2 0.0 copy-start
  7.2 0.8 compare_select_fusion.2
  8.0 0.1 copy.19
  8.1 0.1 reshape.249
  8.2 0.0 copy-done.2
  8.2 29.2 %gather_fusion = bf16[8192,128]{1,0:T(8,128)(2,1)} fusion(bf16[512,128]{1,0:T(8,128)(2,1)S(1)} %copy-done.2, s32[8192]{0:T(1024)S(1)} %broadcast_clamp_fusion), kind=kCustom, calls=%fused_computation | custom fusion | bytes 4227072 | tf_op jit(solution)/shard_map/gather | solution.py:80
  37.5 16.5 %all-to-all-start = ((bf16[128,64,128]{2,1,0:T(8,128)(2,1)}), bf16[128,64,128]{2,1,0:T(8,128)(2,1)S(1)}, u32[]{:S(2)}, u32[]{:S(2)}) async-start(bf16[128,64,128]{2,1,0:T(8,128)(2,1)} %bitcast.1), calls=%async_computation | async-start | bytes 4194304 | tf_op jit(solution)/shard_map/all_to_all | solution.py:80
  53.9 0.1 slice_reduce_fusion.3
  54.1 0.1 slice_reduce_fusion.1
  54.2 0.1 broadcast_subtract_fusion.1
  54.3 0.5 select_reduce_fusion
  55.0 48.3 %all-to-all-done = bf16[128,64,128]{2,1,0:T(8,128)(2,1)S(1)} async-done(((bf16[128,64,128]{2,1,0:T(8,128)(2,1)}), bf16[128,64,128]{2,1,0:T(8,128)(2,1)S(1)}, u32[]{:S(2)}, u32[]{:S(2)}) %all-to-all-start) | async-done | bytes 2097184 | tf_op jit(solution)/shard_map/all_to_all | solution.py:80
  103.3 1.3 copy-done.3
  104.6 1.8 pad_maximum_fusion.2
  106.5 14.9 %gather_fusion.1 = bf16[4096,128]{1,0:T(8,128)(2,1)} fusion(bf16[8704,128]{1,0:T(8,128)(2,1)S(1)} %pad_maximum_fusion.2, s32[4096]{0:T(1024)S(1)} %broadcast_clamp_fusion.2), kind=kCustom, calls=%fused_computation.1 | custom fusion | bytes 2113536 | tf_op jit(solution)/shard_map/gather | solution.py:67
  121.4 2.5 fusion.6
  123.9 14.9 %gather_fusion.2 = bf16[4096,128]{1,0:T(8,128)(2,1)} fusion(bf16[8704,128]{1,0:T(8,128)(2,1)S(1)} %pad_maximum_fusion.2, s32[4096]{0:T(1024)S(1)} %broadcast_clamp_fusion.1), kind=kCustom, calls=%fused_computation.2 | custom fusion | bytes 2113536 | tf_op jit(solution)/shard_map/gather | solution.py:67
  138.8 2.5 fusion.2
  141.3 0.4 fusion.13
  141.7 0.4 fusion.12
  142.2 0.1 pad_maximum_fusion.4
  142.2 0.1 broadcast_in_dim.6
  142.3 8.2 %all_to_all.20 = bf16[2,2,512,256]{3,2,1,0:T(8,128)(2,1)S(1)} all-to-all(bf16[2,2,512,256]{3,2,1,0:T(8,128)(2,1)S(1)} %broadcast_in_dim.6), channel_id=1, replica_groups=mesh['nodes_0'=4,'nodes_1'=8,'nodes_2'=4,'feat'=2] {'feat'}, dimensions={0} | all-to-all | bytes 2097152 | tf_op jit(solution)/shard_map/all_to_all | solution.py:19
  150.5 0.1 copy.28
  150.6 0.4 convolution_convert_fusion
  151.0 0.5 copy.21
  151.6 63.9 %gather_fusion.3 = bf16[8192,2,256]{2,1,0:T(2,128)(2,1)} fusion(bf16[2,512,256]{2,0,1:T(2,128)(2,1)S(1)} %copy.21, s32[8192]{0:T(1024)S(1)} %broadcast_clamp_fusion), kind=kCustom, calls=%fused_computation.3 | custom fusion | bytes 16809984 | tf_op jit(solution)/shard_map/gather | solution.py:96
  215.5 8.6 %copy.30 = bf16[128,64,2,256]{3,1,2,0:T(8,128)(2,1)} copy(bf16[128,64,2,256]{3,2,1,0:T(2,128)(2,1)} %bitcast.76) | data formatting | bytes 16777216 | tf_op jit(solution)/shard_map/gather | solution.py:96
  224.0 7.7 %all-to-all-start.2 = ((bf16[2,128,64,256]{3,2,0,1:T(8,128)(2,1)}), bf16[2,128,64,256]{3,2,0,1:T(8,128)(2,1)}, u32[]{:S(2)}, u32[]{:S(2)}) async-start(bf16[2,128,64,256]{3,2,0,1:T(8,128)(2,1)} %bitcast.75), calls=%async_computation.2 | async-start | bytes 16777216 | tf_op jit(solution)/shard_map/all_to_all | solution.py:95
  231.7 0.0 reduce-scatter.3.cloned.1.call-start
  232.4 180.0 %all-to-all-done.2 = bf16[2,128,64,256]{3,2,0,1:T(8,128)(2,1)} async-done(((bf16[2,128,64,256]{3,2,0,1:T(8,128)(2,1)}), bf16[2,128,64,256]{3,2,0,1:T(8,128)(2,1)}, u32[]{:S(2)}, u32[]{:S(2)}) %all-to-all-start.2) | async-done | bytes 8388640 | tf_op jit(solution)/shard_map/all_to_all | solution.py:95
  412.5 5.3 fusion.41
  417.8 2.8 pad_maximum_fusion.1
  420.6 15.8 %gather_fusion.5 = bf16[4096,256]{1,0:T(8,128)(2,1)S(1)} fusion(bf16[8704,256]{1,0:T(8,128)(2,1)} %pad_maximum_fusion.1, s32[4096]{0:T(1024)S(1)} %broadcast_clamp_fusion.1), kind=kCustom, calls=%fused_computation.5 | custom fusion | bytes 4210688 | tf_op jit(solution)/shard_map/gather | solution.py:67
  436.5 2.1 fusion
  438.5 4.0 pad_maximum_fusion
  442.6 15.8 %gather_fusion.4 = bf16[4096,256]{1,0:T(8,128)(2,1)S(1)} fusion(bf16[8704,256]{1,0:T(8,128)(2,1)} %pad_maximum_fusion, s32[4096]{0:T(1024)S(1)} %broadcast_clamp_fusion.2), kind=kCustom, calls=%fused_computation.4 | custom fusion | bytes 4210688 | tf_op jit(solution)/shard_map/gather | solution.py:67
  458.4 0.0 copy-start.5
  458.4 1.3 fusion.4
  459.7 0.2 fusion.27
  459.9 0.2 multiply_reduce_fusion
  460.2 8.5 %all-reduce.3 = (f32[2,256]{1,0:T(2,128)S(1)}, f32[]{:T(128)}, f32[2,256]{1,0:T(2,128)S(1)}) all-reduce(f32[2,256]{1,0:T(2,128)S(1)} %get-tuple-element.4, f32[]{:T(128)S(6)} %convert_element_type.49, f32[2,256]{1,0:T(2,128)S(1)} %get-tuple-element.3), channel_id=1, replica_groups=mesh['nodes_0'=4,'nodes_1'=8,'nodes_2'=4,'feat'=2] {'nodes_0'}, use_global_device_ids=true, to_apply=%region_3.4 | all-reduce | flops 1025 | bytes 8200 | tf_op jit(solution)/shard_map/psum | solution.py:30
  468.7 16.1 %all-reduce.1 = (f32[2,256]{1,0:T(2,128)S(1)}, f32[]{:T(128)}, f32[2,256]{1,0:T(2,128)S(1)}) all-reduce(f32[2,256]{1,0:T(2,128)S(1)} %get-tuple-element.15, f32[]{:T(128)} %get-tuple-element.16, f32[2,256]{1,0:T(2,128)S(1)} %get-tuple-element.17), channel_id=1, replica_groups=mesh['nodes_0'=4,'nodes_1'=8,'nodes_2'=4,'feat'=2] {'nodes_1'}, use_global_device_ids=true, to_apply=%region_4.5 | all-reduce | flops 1025 | bytes 8200 | tf_op jit(solution)/shard_map/psum | solution.py:30
  484.7 9.1 %all-reduce.2 = (f32[2,256]{1,0:T(2,128)S(1)}, f32[]{:T(128)}, f32[2,256]{1,0:T(2,128)S(1)}) all-reduce(f32[2,256]{1,0:T(2,128)S(1)} %get-tuple-element.9, f32[]{:T(128)} %get-tuple-element.10, f32[2,256]{1,0:T(2,128)S(1)} %get-tuple-element.11), channel_id=1, replica_groups=mesh['nodes_0'=4,'nodes_1'=8,'nodes_2'=4,'feat'=2] {'nodes_2'}, use_global_device_ids=true, to_apply=%region_5.6 | all-reduce | flops 1025 | bytes 8200 | tf_op jit(solution)/shard_map/psum | solution.py:30
  493.8 0.7 add_sqrt_fusion
  494.5 0.2 multiply_convert_fusion
  494.6 0.0 copy-start.4
  494.7 0.0 copy-start.11
  494.7 0.0 copy-start.1
  494.7 0.1 copy.25
  494.9 12.1 %all_to_all.21 = bf16[2,512,256]{1,2,0:T(8,128)(2,1)S(1)} all-to-all(bf16[2,512,256]{1,2,0:T(8,128)(2,1)S(1)} %broadcast_in_dim.8), channel_id=1, replica_groups=mesh['nodes_0'=4,'nodes_1'=8,'nodes_2'=4,'feat'=2] {'feat'}, dimensions={0} | all-to-all | bytes 1048576 | tf_op jit(solution)/shard_map/all_to_all | solution.py:19
  507.0 1.1 fusion.32
  508.1 0.0 reduce-scatter.3.cloned.1.call-update
  508.1 0.0 reduce-scatter.5.cloned.1.call-start
  508.2 16.2 %reduce-scatter.3.cloned.1.call-done = f32[128,256]{1,0:T(8,128)} async-done(((f32[512,256]{1,0:T(8,128)}), f32[128,256]{1,0:T(8,128)}) %reduce-scatter.3.cloned.1.call-update) | async-done | bytes 131088 | tf_op jit(solution)/shard_map/reduce_scatter | solution.py:36
  524.4 0.0 reduce-scatter.5.cloned.1.call-update
  524.4 0.6 dynamic-slice
  525.7 34.7 %reduce-scatter.5.cloned.1.call-done = f32[16,256]{1,0:T(8,128)} async-done(((f32[128,256]{1,0:T(8,128)}), f32[16,256]{1,0:T(8,128)}) %reduce-scatter.5.cloned.1.call-update) | async-done | bytes 16400 | tf_op jit(solution)/shard_map/reduce_scatter | solution.py:36
  560.5 13.7 %all-reduce = f32[16,256]{1,0:T(8,128)S(1)} all-reduce(f32[16,256]{1,0:T(8,128)} %reduce-scatter.5.cloned.1.call-done), channel_id=4, replica_groups=mesh['nodes_0'=4,'nodes_1'=8,'nodes_2'=4,'feat'=2] {'nodes_2'}, use_global_device_ids=true, to_apply=%region_15.16.clone | all-reduce | flops 4096 | bytes 32768
  574.2 1.9 select_reduce_fusion.2
  576.1 9.0 %psum.100 = f32[]{:T(128)} all-reduce(f32[]{:T(128)} %get-tuple-element.18), channel_id=1, replica_groups=mesh['nodes_0'=4,'nodes_1'=8,'nodes_2'=4,'feat'=2] {'nodes_0'}, use_global_device_ids=true, to_apply=%region_17.18 | all-reduce | flops 1 | bytes 8 | tf_op jit(solution)/shard_map/psum | solution.py:30
  585.1 12.6 %psum.101 = f32[]{:T(128)} all-reduce(f32[]{:T(128)} %psum.100), channel_id=1, replica_groups=mesh['nodes_0'=4,'nodes_1'=8,'nodes_2'=4,'feat'=2] {'nodes_1'}, use_global_device_ids=true, to_apply=%region_18.19 | all-reduce | flops 1 | bytes 8 | tf_op jit(solution)/shard_map/psum | solution.py:30
  597.7 6.6 %psum.102 = f32[]{:T(128)} all-reduce(f32[]{:T(128)} %psum.101), channel_id=1, replica_groups=mesh['nodes_0'=4,'nodes_1'=8,'nodes_2'=4,'feat'=2] {'nodes_2'}, use_global_device_ids=true, to_apply=%region_19.20 | all-reduce | flops 1 | bytes 8 | tf_op jit(solution)/shard_map/psum | solution.py:30
  604.3 19.9 %psum.103 = f32[]{:T(128)} all-reduce(f32[]{:T(128)} %psum.102), channel_id=1, replica_groups=mesh['nodes_0'=4,'nodes_1'=8,'nodes_2'=4,'feat'=2] {'feat'}, use_global_device_ids=true, to_apply=%region_20.21 | all-reduce | flops 1 | bytes 8 | tf_op jit(solution)/shard_map/psum | solution.py:30
  (35 shorter events, 0.3 us)
Async XLA Ops:
  7.2 143.4 %copy-start = (bf16[512,256]{1,0:T(8,128)(2,1)S(1)}, bf16[512,256]{1,0:T(8,128)(2,1)}, u32[]{:S(2)}) copy-start(bf16[512,256]{1,0:T(8,128)(2,1)} %param.17) | copy-start | bytes 786436
  7.2 1.0 copy-start.2
  37.5 16.5 %copy-start.6 = (s32[2,4096]{1,0:T(2,128)S(1)}, s32[2,4096]{1,0:T(2,128)}, u32[]{:S(2)}) copy-start(s32[2,4096]{1,0:T(2,128)} %param.13) | copy-start | bytes 98308
  37.5 16.6 %copy-start.7 = (s32[2,4096]{1,0:T(2,128)S(1)}, s32[2,4096]{1,0:T(2,128)}, u32[]{:S(2)}) copy-start(s32[2,4096]{1,0:T(2,128)} %param.14) | copy-start | bytes 98308
  37.5 17.4 %copy-start.8 = (s32[2,4096]{1,0:T(2,128)S(1)}, s32[2,4096]{1,0:T(2,128)}, u32[]{:S(2)}) copy-start(s32[2,4096]{1,0:T(2,128)} %param.12) | copy-start | bytes 98308
  37.5 65.8 %all-to-all-start = ((bf16[128,64,128]{2,1,0:T(8,128)(2,1)}), bf16[128,64,128]{2,1,0:T(8,128)(2,1)S(1)}, u32[]{:S(2)}, u32[]{:S(2)}) async-start(bf16[128,64,128]{2,1,0:T(8,128)(2,1)} %bitcast.1), calls=%async_computation | async-start | bytes 4194304 | tf_op jit(solution)/shard_map/all_to_all | solution.py:80
  103.3 1.4 copy-start.3
  138.7 2.5 copy-start.9
  138.8 2.5 copy-start.10
  224.0 188.5 %all-to-all-start.2 = ((bf16[2,128,64,256]{3,2,0,1:T(8,128)(2,1)}), bf16[2,128,64,256]{3,2,0,1:T(8,128)(2,1)}, u32[]{:S(2)}, u32[]{:S(2)}) async-start(bf16[2,128,64,256]{3,2,0,1:T(8,128)(2,1)} %bitcast.75), calls=%async_computation.2 | async-start | bytes 16777216 | tf_op jit(solution)/shard_map/all_to_all | solution.py:95
  231.7 292.7 %reduce-scatter.3.cloned.1.call-start = ((), (), s32[]{:S(2)}) async-start(), calls=%async_computation.6 | async-start | bytes 655360 | tf_op jit(solution)/shard_map/reduce_scatter | solution.py:36
  458.4 1.3 copy-start.5
  494.6 13.5 %copy-start.4 = (bf16[2,512,256]{2,1,0:T(8,128)(2,1)}, bf16[2,512,256]{2,1,0:T(8,128)(2,1)S(1)}, u32[]{:S(2)}) copy-start(bf16[2,512,256]{2,1,0:T(8,128)(2,1)S(1)} %multiply_convert_fusion) | copy-start | bytes 1572868
  494.7 29.8 %copy-start.11 = (u32[256]{0:T(256)S(1)}, u32[256]{0:T(256)}, u32[]{:S(2)}) copy-start(u32[256]{0:T(256)} %constant.49) | copy-start | bytes 3076
  494.7 129.6 %copy-start.1 = (bf16[512,256]{1,0:T(8,128)(2,1)S(1)}, bf16[512,256]{1,0:T(8,128)(2,1)}, u32[]{:S(2)}) copy-start(bf16[512,256]{1,0:T(8,128)(2,1)} %param.17) | copy-start | bytes 786436
  508.1 52.3 %reduce-scatter.5.cloned.1.call-start = ((), (), s32[]{:S(2)}) async-start(), calls=%async_computation.7 | async-start | bytes 147456 | tf_op jit(solution)/shard_map/reduce_scatter | solution.py:36
Sparse Core Ops, SparseCore 0:
  508.3 16.0 reduce-scatter.2
  526.9 33.5 reduce-scatter.4
where the time goes:
time: 632 us; the launch traced here: 631 us
  waiting for transfers between devices  279 us (44%)
  local copies, waits for them, and re-layouts  172 us (27%)
  blocking collectives  116 us (18%)
  starting transfers between devices  24.2 us (4%)
  between operations  15.8 us (2%)
  other arithmetic  13.5 us (2%)
  matrix products  10.7 us (2%)
    all_to_all x1, waiting for transfers between devices, per_device(): lax.all_to_all(projected[:, outbound], NODES, split_axis=1, concat_axis=1...  180 us
    psum x7, blocking collectives, over_axes(): shard = lax.psum(shard, axis)  81.8 us
    gather x2, local copies, waits for them, and re-layouts, per_device(): projected[:, outbound]  72.5 us
    gather x4, local copies, waits for them, and re-layouts, mix_view(): lookup[edge_src[view_index]].astype(jnp.float32)  61.4 us
    reduce_scatter x2, waiting for transfers between devices, own_rows(): running = lax.psum_scatter(running, axis, scatter_dimension=0, tiled=True)  51 us
    all_to_all x1, waiting for transfers between devices, per_device(): lax.all_to_all(features[outbound], NODES, split_axis=0, concat_axis=0, ti...  48.3 us
    gather x1, local copies, waits for them, and re-layouts, per_device(): features[outbound]  29.2 us
    all_to_all x2, blocking collectives, from_everyone(): lax.all_to_all(jnp.broadcast_to(shard[None], (devices, *shard.shape)), ax...  20.3 us
  transfers between devices with their start and end apart: 4, of which 4 were waited for; matrix products, arithmetic and copies ran while one was open for 0% of the time, Pallas kernels for 0%

commit v1 on v0

--- a/solution.py
+++ b/solution.py
@@ -27,7 +27,7 @@
 
 def over_axes(shard, axes):
     for axis in axes:
-        shard = lax.psum(shard, axis)
+        shard = jnp.sum(lax.all_gather(shard, axis), axis=0)
     return shard
 
 

time: 632 us -> 711 us (1.12)
  blocking collectives: 116 us -> 356 us
  waiting for transfers between devices: 279 us -> 103 us
  local copies, waits for them, and re-layouts: 172 us -> 183 us
    unnamed x1 -> x8, blocking collectives: 13.7 us -> 252 us
    all_to_all x1, waiting for transfers between devices: 180 us -> 0.01 us  [per_device(): lax.all_to_all(projected[:, outbound], NODES, split_axis=1, concat_axis=1...]
    psum x7 -> x0, blocking collectives: 81.8 us -> none  [over_axes(): shard = lax.psum(shard, axis)]
    all_gather x0 -> x6, blocking collectives: none -> 64.7 us  [over_axes(): shard = jnp.sum(lax.all_gather(shard, axis), axis=0)]
    all_to_all x2, blocking collectives: 20.3 us -> 39.7 us  [from_everyone(): lax.all_to_all(jnp.broadcast_to(shard[None], (devices, *shard.shape)), ax...]
    unnamed x25 -> x48, local copies, waits for them, and re-layouts: 2 us -> 13 us
  transfers between devices with their start and end apart: 4 -> 4, of which waited for: 4 -> 3; matrix products, arithmetic and copies ran while one was open for 0% -> 1% of each run, Pallas kernels for 0% -> 0%
where the time goes in v1:
time: 711 us; the launch traced here: 710 us
  blocking collectives  356 us (50%)
  local copies, waits for them, and re-layouts  183 us (26%)
  waiting for transfers between devices  103 us (14%)
  starting transfers between devices  24.3 us (3%)
  other arithmetic  17.7 us (2%)
  between operations  15.8 us (2%)
  matrix products  10.7 us (2%)
    unnamed x8, blocking collectives  252 us
    gather x2, local copies, waits for them, and re-layouts, per_device(): projected[:, outbound]  72.5 us
    all_gather x6, blocking collectives, over_axes(): shard = jnp.sum(lax.all_gather(shard, axis), axis=0)  64.7 us
    gather x4, local copies, waits for them, and re-layouts, mix_view(): lookup[edge_src[view_index]].astype(jnp.float32)  61.4 us
    reduce_scatter x2, waiting for transfers between devices, own_rows(): running = lax.psum_scatter(running, axis, scatter_dimension=0, tiled=True)  54.4 us
    all_to_all x1, waiting for transfers between devices, per_device(): lax.all_to_all(features[outbound], NODES, split_axis=0, concat_axis=0, ti...  48.3 us
    all_to_all x2, blocking collectives, from_everyone(): lax.all_to_all(jnp.broadcast_to(shard[None], (devices, *shard.shape)), ax...  39.7 us
    gather x1, local copies, waits for them, and re-layouts, per_device(): features[outbound]  29.2 us
  transfers between devices with their start and end apart: 4, of which 3 were waited for; matrix products, arithmetic and copies ran while one was open for 1% of the time, Pallas kernels for 0%

profile of v1, /device:TPU:1, one launch (start us, length us, event | category | flops | bytes accessed | tf_op | source)
XLA Modules:
  0.0 710.0 jit_solution(10667455482702117308)
XLA Ops:
  7.2 0.8 compare_select_fusion.2
  8.2 29.2 %gather_fusion = bf16[8192,128]{1,0:T(8,128)(2,1)} fusion(bf16[512,128]{1,0:T(8,128)(2,1)S(1)} %copy-done.2, s32[8192]{0:T(1024)S(1)} %broadcast_clamp_fusion), kind=kCustom, calls=%fused_computation | custom fusion | bytes 4227072 | tf_op jit(solution)/shard_map/gather | solution.py:80
  37.5 16.5 %all-to-all-start = ((bf16[128,64,128]{2,1,0:T(8,128)(2,1)}), bf16[128,64,128]{2,1,0:T(8,128)(2,1)S(1)}, u32[]{:S(2)}, u32[]{:S(2)}) async-start(bf16[128,64,128]{2,1,0:T(8,128)(2,1)} %bitcast.1), calls=%async_computation | async-start | bytes 4194304 | tf_op jit(solution)/shard_map/all_to_all | solution.py:80
  54.3 0.5 select_reduce_fusion
  55.0 48.3 %all-to-all-done = bf16[128,64,128]{2,1,0:T(8,128)(2,1)S(1)} async-done(((bf16[128,64,128]{2,1,0:T(8,128)(2,1)}), bf16[128,64,128]{2,1,0:T(8,128)(2,1)S(1)}, u32[]{:S(2)}, u32[]{:S(2)}) %all-to-all-start) | async-done | bytes 2097184 | tf_op jit(solution)/shard_map/all_to_all | solution.py:80
  103.3 1.3 copy-done.3
  104.6 1.8 pad_maximum_fusion.2
  106.5 14.9 %gather_fusion.1 = bf16[4096,128]{1,0:T(8,128)(2,1)} fusion(bf16[8704,128]{1,0:T(8,128)(2,1)S(1)} %pad_maximum_fusion.2, s32[4096]{0:T(1024)S(1)} %broadcast_clamp_fusion.2), kind=kCustom, calls=%fused_computation.1 | custom fusion | bytes 2113536 | tf_op jit(solution)/shard_map/gather | solution.py:67
  121.4 2.5 fusion.6
  123.9 14.9 %gather_fusion.2 = bf16[4096,128]{1,0:T(8,128)(2,1)} fusion(bf16[8704,128]{1,0:T(8,128)(2,1)S(1)} %pad_maximum_fusion.2, s32[4096]{0:T(1024)S(1)} %broadcast_clamp_fusion.1), kind=kCustom, calls=%fused_computation.2 | custom fusion | bytes 2113536 | tf_op jit(solution)/shard_map/gather | solution.py:67
  138.8 2.5 fusion.2
  141.3 0.4 fusion.13
  141.7 0.4 fusion.12
  142.3 8.2 %all_to_all.20 = bf16[2,2,512,256]{3,2,1,0:T(8,128)(2,1)S(1)} all-to-all(bf16[2,2,512,256]{3,2,1,0:T(8,128)(2,1)S(1)} %broadcast_in_dim.6), channel_id=1, replica_groups=mesh['nodes_0'=4,'nodes_1'=8,'nodes_2'=4,'feat'=2] {'feat'}, dimensions={0} | all-to-all | bytes 2097152 | tf_op jit(solution)/shard_map/all_to_all | solution.py:19
  150.6 0.4 convolution_convert_fusion
  151.0 0.5 copy.21
  151.6 63.9 %gather_fusion.3 = bf16[8192,2,256]{2,1,0:T(2,128)(2,1)} fusion(bf16[2,512,256]{2,0,1:T(2,128)(2,1)S(1)} %copy.21, s32[8192]{0:T(1024)S(1)} %broadcast_clamp_fusion), kind=kCustom, calls=%fused_computation.3 | custom fusion | bytes 16809984 | tf_op jit(solution)/shard_map/gather | solution.py:96
  215.5 8.6 %copy.30 = bf16[128,64,2,256]{3,1,2,0:T(8,128)(2,1)} copy(bf16[128,64,2,256]{3,2,1,0:T(2,128)(2,1)} %bitcast.93) | data formatting | bytes 16777216 | tf_op jit(solution)/shard_map/gather | solution.py:96
  224.0 7.8 %all-to-all-start.2 = ((bf16[2,128,64,256]{3,2,0,1:T(8,128)(2,1)}), bf16[2,128,64,256]{3,2,0,1:T(8,128)(2,1)}, u32[]{:S(2)}, u32[]{:S(2)}) async-start(bf16[2,128,64,256]{3,2,0,1:T(8,128)(2,1)} %bitcast.92), calls=%async_computation.2 | async-start | bytes 16777216 | tf_op jit(solution)/shard_map/all_to_all | solution.py:95
  232.5 0.6 dynamic-slice
  233.1 0.7 dynamic-update-slice
  233.8 13.6 %all-reduce = f32[4]{0:T(128)S(1)} all-reduce(f32[4]{0:T(128)S(1)} %dynamic-update-slice), channel_id=1, replica_groups=mesh['nodes_0'=4,'nodes_1'=8,'nodes_2'=4,'feat'=2] {'nodes_0'}, use_global_device_ids=true, to_apply=%add | all-reduce | flops 4 | bytes 32
  247.4 0.7 dynamic-slice.1
  248.0 0.6 reduce_sum.168
  248.6 1.4 dynamic-update-slice.1
  250.1 170.6 %all-reduce.1 = f32[8]{0:T(128)S(1)} all-reduce(f32[8]{0:T(128)S(1)} %dynamic-update-slice.1), channel_id=1, replica_groups=mesh['nodes_0'=4,'nodes_1'=8,'nodes_2'=4,'feat'=2] {'nodes_1'}, use_global_device_ids=true, to_apply=%add.1 | all-reduce | flops 8 | bytes 64
  420.7 0.6 reduce_sum.169
  421.3 0.6 fusion.42
  421.9 1.4 dynamic-update-slice.2
  423.3 8.0 %all-reduce.2 = f32[4]{0:T(128)S(1)} all-reduce(f32[4]{0:T(128)S(1)} %dynamic-update-slice.2), channel_id=1, replica_groups=mesh['nodes_0'=4,'nodes_1'=8,'nodes_2'=4,'feat'=2] {'nodes_2'}, use_global_device_ids=true, to_apply=%add.2 | all-reduce | flops 4 | bytes 32
  431.3 0.6 reduce_sum.170
  432.0 5.3 fusion.41
  437.3 2.8 pad_maximum_fusion.1
  440.1 15.8 %gather_fusion.5 = bf16[4096,256]{1,0:T(8,128)(2,1)S(1)} fusion(bf16[8704,256]{1,0:T(8,128)(2,1)} %pad_maximum_fusion.1, s32[4096]{0:T(1024)S(1)} %broadcast_clamp_fusion.1), kind=kCustom, calls=%fused_computation.5 | custom fusion | bytes 4210688 | tf_op jit(solution)/shard_map/gather | solution.py:67
  456.0 2.1 fusion
  458.0 4.0 pad_maximum_fusion
  462.1 15.8 %gather_fusion.4 = bf16[4096,256]{1,0:T(8,128)(2,1)S(1)} fusion(bf16[8704,256]{1,0:T(8,128)(2,1)} %pad_maximum_fusion, s32[4096]{0:T(1024)S(1)} %broadcast_clamp_fusion.2), kind=kCustom, calls=%fused_computation.4 | custom fusion | bytes 4210688 | tf_op jit(solution)/shard_map/gather | solution.py:67
  477.9 1.3 fusion.4
  479.7 8.7 %all-gather.6 = f32[4,2,256]{2,1,0:T(2,128)S(1)} all-gather(f32[1,2,256]{2,1,0:T(2,128)S(1)} %bitcast.109), channel_id=2, replica_groups=mesh['nodes_0'=4,'nodes_1'=8,'nodes_2'=4,'feat'=2] {'nodes_0'}, dimensions={0}, use_global_device_ids=true | all-gather | bytes 10240 | tf_op jit(solution)/shard_map/all_gather | solution.py:30
  488.4 16.0 %all-gather.7 = f32[8,2,256]{2,1,0:T(2,128)S(1)} all-gather(f32[1,2,256]{2,1,0:T(2,128)S(1)} %bitcast.112), channel_id=3, replica_groups=mesh['nodes_0'=4,'nodes_1'=8,'nodes_2'=4,'feat'=2] {'nodes_1'}, dimensions={0}, use_global_device_ids=true | all-gather | bytes 18432 | tf_op jit(solution)/shard_map/all_gather | solution.py:30
  504.4 8.1 %all-gather.8 = f32[4,2,256]{2,1,0:T(2,128)S(1)} all-gather(f32[1,2,256]{2,1,0:T(2,128)S(1)} %bitcast.110), channel_id=4, replica_groups=mesh['nodes_0'=4,'nodes_1'=8,'nodes_2'=4,'feat'=2] {'nodes_2'}, dimensions={0}, use_global_device_ids=true | all-gather | bytes 10240 | tf_op jit(solution)/shard_map/all_gather | solution.py:30
  512.5 8.1 %all-gather.9 = f32[4,2,256]{2,1,0:T(2,128)S(1)} all-gather(f32[1,2,256]{2,1,0:T(2,128)S(1)} %bitcast.108), channel_id=5, replica_groups=mesh['nodes_0'=4,'nodes_1'=8,'nodes_2'=4,'feat'=2] {'nodes_0'}, dimensions={0}, use_global_device_ids=true | all-gather | bytes 10240 | tf_op jit(solution)/shard_map/all_gather | solution.py:30
  520.7 15.6 %all-gather.10 = f32[8,2,256]{2,1,0:T(2,128)S(1)} all-gather(f32[1,2,256]{2,1,0:T(2,128)S(1)} %bitcast.113), channel_id=6, replica_groups=mesh['nodes_0'=4,'nodes_1'=8,'nodes_2'=4,'feat'=2] {'nodes_1'}, dimensions={0}, use_global_device_ids=true | all-gather | bytes 18432 | tf_op jit(solution)/shard_map/all_gather | solution.py:30
  536.3 8.1 %all-gather.11 = f32[4,2,256]{2,1,0:T(2,128)S(1)} all-gather(f32[1,2,256]{2,1,0:T(2,128)S(1)} %bitcast.111), channel_id=7, replica_groups=mesh['nodes_0'=4,'nodes_1'=8,'nodes_2'=4,'feat'=2] {'nodes_2'}, dimensions={0}, use_global_device_ids=true | all-gather | bytes 10240 | tf_op jit(solution)/shard_map/all_gather | solution.py:30
  544.4 0.6 add_sqrt_fusion
  545.5 31.5 %all_to_all.21 = bf16[2,512,256]{1,2,0:T(8,128)(2,1)S(1)} all-to-all(bf16[2,512,256]{1,2,0:T(8,128)(2,1)S(1)} %broadcast_in_dim.8), channel_id=1, replica_groups=mesh['nodes_0'=4,'nodes_1'=8,'nodes_2'=4,'feat'=2] {'feat'}, dimensions={0} | all-to-all | bytes 1048576 | tf_op jit(solution)/shard_map/all_to_all | solution.py:19
  577.0 1.1 fusion.32
  578.2 19.0 %reduce-scatter.3.cloned.1.call-done = f32[128,256]{1,0:T(8,128)} async-done(((f32[512,256]{1,0:T(8,128)}), f32[128,256]{1,0:T(8,128)}) %reduce-scatter.3.cloned.1.call-update) | async-done | bytes 131088 | tf_op jit(solution)/shard_map/reduce_scatter | solution.py:36
  597.9 35.4 %reduce-scatter.5.cloned.1.call-done = f32[16,256]{1,0:T(8,128)} async-done(((f32[128,256]{1,0:T(8,128)}), f32[16,256]{1,0:T(8,128)}) %reduce-scatter.5.cloned.1.call-update) | async-done | bytes 16400 | tf_op jit(solution)/shard_map/reduce_scatter | solution.py:36
  633.3 13.6 %all-reduce.7 = f32[16,256]{1,0:T(8,128)S(1)} all-reduce(f32[16,256]{1,0:T(8,128)} %reduce-scatter.5.cloned.1.call-done), channel_id=10, replica_groups=mesh['nodes_0'=4,'nodes_1'=8,'nodes_2'=4,'feat'=2] {'nodes_2'}, use_global_device_ids=true, to_apply=%region_15.16.clone | all-reduce | flops 4096 | bytes 32768
  646.9 1.8 select_reduce_fusion.2
  648.8 1.3 dynamic-update-slice.3
  650.1 8.4 %all-reduce.3 = f32[4]{0:T(128)S(1)} all-reduce(f32[4]{0:T(128)S(1)} %dynamic-update-slice.3), channel_id=1, replica_groups=mesh['nodes_0'=4,'nodes_1'=8,'nodes_2'=4,'feat'=2] {'nodes_0'}, use_global_device_ids=true, to_apply=%add.3 | all-reduce | flops 4 | bytes 32
  658.5 0.6 reduce_sum.176
  659.1 1.4 dynamic-update-slice.4
  660.6 12.0 %all-reduce.4 = f32[8]{0:T(128)S(1)} all-reduce(f32[8]{0:T(128)S(1)} %dynamic-update-slice.4), channel_id=1, replica_groups=mesh['nodes_0'=4,'nodes_1'=8,'nodes_2'=4,'feat'=2] {'nodes_1'}, use_global_device_ids=true, to_apply=%add.4 | all-reduce | flops 8 | bytes 64
  672.6 0.6 reduce_sum.177
  673.2 1.4 dynamic-update-slice.5
  674.5 0.7 dynamic-slice.6
  675.2 6.1 all-reduce.5
  681.2 0.6 reduce_sum.178
  681.9 1.4 dynamic-update-slice.6
  683.3 19.3 %all-reduce.6 = f32[2]{0:T(128)S(1)} all-reduce(f32[2]{0:T(128)S(1)} %dynamic-update-slice.6), channel_id=1, replica_groups=mesh['nodes_0'=4,'nodes_1'=8,'nodes_2'=4,'feat'=2] {'feat'}, use_global_device_ids=true, to_apply=%add.6 | all-reduce | flops 2 | bytes 16
  702.6 0.6 reduce_sum.179
  (77 shorter events, 1.9 us)
Async XLA Ops:
  7.2 143.4 %copy-start = (bf16[512,256]{1,0:T(8,128)(2,1)S(1)}, bf16[512,256]{1,0:T(8,128)(2,1)}, u32[]{:S(2)}) copy-start(bf16[512,256]{1,0:T(8,128)(2,1)} %param.17) | copy-start | bytes 786436
  7.2 1.0 copy-start.2
  37.5 16.5 %copy-start.6 = (s32[2,4096]{1,0:T(2,128)S(1)}, s32[2,4096]{1,0:T(2,128)}, u32[]{:S(2)}) copy-start(s32[2,4096]{1,0:T(2,128)} %param.13) | copy-start | bytes 98308
  37.5 16.6 %copy-start.7 = (s32[2,4096]{1,0:T(2,128)S(1)}, s32[2,4096]{1,0:T(2,128)}, u32[]{:S(2)}) copy-start(s32[2,4096]{1,0:T(2,128)} %param.14) | copy-start | bytes 98308
  37.5 17.4 %copy-start.8 = (s32[2,4096]{1,0:T(2,128)S(1)}, s32[2,4096]{1,0:T(2,128)}, u32[]{:S(2)}) copy-start(s32[2,4096]{1,0:T(2,128)} %param.12) | copy-start | bytes 98308
  37.5 65.8 %all-to-all-start = ((bf16[128,64,128]{2,1,0:T(8,128)(2,1)}), bf16[128,64,128]{2,1,0:T(8,128)(2,1)S(1)}, u32[]{:S(2)}, u32[]{:S(2)}) async-start(bf16[128,64,128]{2,1,0:T(8,128)(2,1)} %bitcast.1), calls=%async_computation | async-start | bytes 4194304 | tf_op jit(solution)/shard_map/all_to_all | solution.py:80
  103.3 1.4 copy-start.3
  138.7 2.5 copy-start.10
  138.8 2.5 copy-start.11
  224.0 8.5 %copy-start.14 = (u32[256]{0:T(256)S(1)}, u32[256]{0:T(256)}, u32[]{:S(2)}) copy-start(u32[256]{0:T(256)} %constant.49) | copy-start | bytes 3076
  224.0 23.4 %copy-start.13 = (u32[256]{0:T(256)S(1)}, u32[256]{0:T(256)}, u32[]{:S(2)}) copy-start(u32[256]{0:T(256)} %constant.54) | copy-start | bytes 3076
  224.0 197.3 %copy-start.9 = (u32[256]{0:T(256)S(1)}, u32[256]{0:T(256)}, u32[]{:S(2)}) copy-start(u32[256]{0:T(256)} %constant.59) | copy-start | bytes 3076
  224.0 207.9 %all-to-all-start.2 = ((bf16[2,128,64,256]{3,2,0,1:T(8,128)(2,1)}), bf16[2,128,64,256]{3,2,0,1:T(8,128)(2,1)}, u32[]{:S(2)}, u32[]{:S(2)}) async-start(bf16[2,128,64,256]{3,2,0,1:T(8,128)(2,1)} %bitcast.92), calls=%async_computation.2 | async-start | bytes 16777216 | tf_op jit(solution)/shard_map/all_to_all | solution.py:95
  231.8 365.3 %reduce-scatter.3.cloned.1.call-start = ((), (), s32[]{:S(2)}) async-start(), calls=%async_computation.6 | async-start | bytes 655360 | tf_op jit(solution)/shard_map/reduce_scatter | solution.py:36
  477.9 1.3 copy-start.5
  545.3 32.9 %copy-start.4 = (bf16[2,512,256]{2,1,0:T(8,128)(2,1)}, bf16[2,512,256]{2,1,0:T(8,128)(2,1)S(1)}, u32[]{:S(2)}) copy-start(bf16[2,512,256]{2,1,0:T(8,128)(2,1)S(1)} %multiply_convert_fusion) | copy-start | bytes 1572868
  545.3 129.2 %copy-start.12 = (u32[256]{0:T(256)S(1)}, u32[256]{0:T(256)}, u32[]{:S(2)}) copy-start(u32[256]{0:T(256)} %constant.79) | copy-start | bytes 3076
  545.3 157.9 %copy-start.1 = (bf16[512,256]{1,0:T(8,128)(2,1)S(1)}, bf16[512,256]{1,0:T(8,128)(2,1)}, u32[]{:S(2)}) copy-start(bf16[512,256]{1,0:T(8,128)(2,1)} %param.17) | copy-start | bytes 786436
  578.1 55.1 %reduce-scatter.5.cloned.1.call-start = ((), (), s32[]{:S(2)}) async-start(), calls=%async_computation.7 | async-start | bytes 147456 | tf_op jit(solution)/shard_map/reduce_scatter | solution.py:36
Sparse Core Ops, SparseCore 0:
  578.3 18.8 reduce-scatter.2
  599.7 33.5 reduce-scatter.4
